TPU v7x, 32 devices: a whole 2x2x4 slice. The times are simulated.
32 devices in a mesh: dp: 8 (over y, x, core), tensor: 4 (over z).
Axes of the slice: x: 2, y: 2, z: 4, core: 2. Of those that a mesh axis runs over, the one named last changes fastest.
Arguments:
- layer_input: bfloat16 [2048, 4096], P(('dp', 'tensor')), parts along dimension 0, may hold values from -6 to 10
- norm_gain: float32 [4096], replicated, may hold values from 0.25 to 1.75
- query_weight: bfloat16 [4096, 4096], P(None, 'tensor'), may hold values from -1 to 1
- key_weight: bfloat16 [4096, 1024], P(None, 'tensor'), may hold values from -1 to 1
- value_matrix: bfloat16 [4096, 1024], P(None, 'tensor'), may hold values from -0.09375 to 0.09375
- output_weight: bfloat16 [4096, 4096], P('tensor'), may hold values from -0.09375 to 0.09375
- keep_bits: int32 [256, 4, 4], P(('dp', 'tensor')), parts along dimension 0, may hold values 0 or 1
Outputs:
- layer_output: bfloat16 [2048, 4096], P(('dp', 'tensor')), parts along dimension 0
There are 8 independent parts, one for each index of `dp`. A program takes and returns all parts, laid end to end along the dimension named above; an argument that names none is the same for every part. Nothing has to cross between parts.
All inputs are finite; a program needn't handle non-finite values. No bound on the sum of `keep_bits` on one device may be relied on, other than what follows from the above.
Results may differ from a plain program's by a relative error of at most 0.0095.
Values may be sent and summed in bfloat16 or wider, within the bound.
A program may use at most 128 MiB of HBM per device.

v0:
```python
import functools

import jax
import jax.numpy as jnp
import numpy as np
from jax import lax
from jax.experimental import pallas as pl
from jax.experimental.pallas import tpu as pltpu
from jax.sharding import PartitionSpec as P

QUERY_HEADS = 32
KEY_VALUE_HEADS = 8
HEAD_SIZE = 128
BLOCK = 64


theta_base = 1000000.0


def as_sent(array):

    def short(part):
        return part.astype(jnp.bfloat16) if part.dtype == jnp.float32 else part

    return jax.tree.map(short, array)


def from_partner(array, axis, distance):
    return lax.ppermute(array, axis, [(i, i ^ 1 << distance) for i in range(lax.axis_size(axis))])


def apply_rotary(block, token_positions):
    half = block.shape[-1] // 2
    freqs = theta_base ** (-(jnp.arange(half, dtype=jnp.float32) * 2.0) / block.shape[-1])
    angles = token_positions[:, None] * freqs[None, :]
    cosine = jnp.cos(angles)
    sine = jnp.sin(angles)
    first = block[..., :half]
    second = block[..., half:]
    return jnp.concatenate(
        [first * cosine - second * sine, second * cosine + first * sine], axis=-1
    )


def join_pairs(mine, other, lowbit):
    ahead = jnp.concatenate([mine, other], axis=-1)
    behind = jnp.concatenate([other, mine], axis=-1)
    return jnp.where(lowbit, ahead, behind)


def attend(query, key_rows, value_rows, keep_bits):
    heads, sequence_length, width = query.shape
    count = min(8, max(1, sequence_length // 512))
    height = sequence_length // count
    divisor = jnp.sqrt(jnp.float32(HEAD_SIZE))
    results = []
    for number in range(count):
        first_row = number * height
        last_row = first_row + height
        scores = (
            jnp.einsum(
                "hqd,hkd->hqk",
                query[:, first_row:last_row],
                key_rows[:, :last_row],
                preferred_element_type=jnp.float32,
            )
            / divisor
        )
        causal = jnp.arange(last_row)[None, :] <= jnp.arange(first_row, last_row)[:, None]
        scores = jnp.where(causal[None], scores, jnp.float32(-1e30))
        highest = jnp.max(scores, axis=-1, keepdims=True)
        expo_terms = jnp.exp(scores - highest)
        weights = expo_terms / jnp.sum(expo_terms, axis=-1, keepdims=True)
        chosen_bits = keep_bits[
            :, first_row // BLOCK : last_row // BLOCK, : last_row // BLOCK
        ].astype(jnp.float32)
        keeper = jnp.broadcast_to(
            chosen_bits[:, :, None, :, None],
            (heads, height // BLOCK, BLOCK, last_row // BLOCK, BLOCK),
        ).reshape(heads, height, last_row)
        dropped = (weights * keeper / 0.9).astype(jnp.bfloat16)
        outcome = jnp.einsum(
            "hqk,hkd->hqd", dropped, value_rows[:, :last_row], preferred_element_type=jnp.float32
        )
        results.append(outcome.astype(jnp.bfloat16))
    return jnp.concatenate(results, axis=1)


def on_device(
    layer_input, norm_gain, query_weight, key_weight, value_matrix, output_weight, keep_bits
):
    devices = lax.axis_size("tensor")
    if 1 < devices <= KEY_VALUE_HEADS // 2 and layer_input.shape[0] == BLOCK:
        return fused(
            layer_input,
            norm_gain,
            query_weight,
            key_weight,
            value_matrix,
            output_weight,
            keep_bits,
        )
    position = lax.axis_index("tensor")
    sharing = devices // KEY_VALUE_HEADS if devices > KEY_VALUE_HEADS else 1
    rounds = sharing.bit_length() - 1
    inputs = layer_input.astype(jnp.float32)
    scaled = lax.rsqrt(jnp.mean(inputs * inputs, axis=-1, keepdims=True) + 1e-05)
    normed = (inputs * scaled * norm_gain[None, :]).astype(jnp.bfloat16)
    query_cols = query_weight.shape[1]
    kv_cols = key_weight.shape[1]
    piece = lax.all_gather(normed, "tensor", axis=0, tiled=True)
    projected = jnp.concatenate(
        [
            jnp.dot(piece, query_weight, preferred_element_type=jnp.float32),
            jnp.dot(piece, key_weight, preferred_element_type=jnp.float32),
            jnp.dot(piece, value_matrix, preferred_element_type=jnp.float32),
        ],
        axis=1,
    )
    query_raw = projected[:, :query_cols]
    paired = jnp.stack(
        [projected[:, query_cols : query_cols + kv_cols], projected[:, query_cols + kv_cols :]]
    ).astype(jnp.bfloat16)
    for level in range(rounds):
        other = from_partner(as_sent(paired), "tensor", level).astype(paired.dtype)
        paired = join_pairs(paired, other, position >> level & 1 == 0)
    sequence_length = query_raw.shape[0]
    local_heads = query_cols // HEAD_SIZE
    local_kv = paired.shape[2] // HEAD_SIZE
    token_positions = jnp.arange(sequence_length).astype(jnp.float32)
    query = apply_rotary(
        query_raw.reshape(sequence_length, local_heads, HEAD_SIZE).transpose(1, 0, 2),
        token_positions,
    ).astype(jnp.bfloat16)
    key_rows = apply_rotary(
        paired[0]
        .astype(jnp.float32)
        .reshape(sequence_length, local_kv, HEAD_SIZE)
        .transpose(1, 0, 2),
        token_positions,
    ).astype(jnp.bfloat16)
    value_rows = paired[1].reshape(sequence_length, local_kv, HEAD_SIZE).transpose(1, 0, 2)
    query_group = QUERY_HEADS // KEY_VALUE_HEADS
    if local_heads >= query_group:
        key_rows = jnp.repeat(key_rows, query_group, axis=0)
        value_rows = jnp.repeat(value_rows, query_group, axis=0)
    else:
        key_rows = jnp.broadcast_to(key_rows, (local_heads, sequence_length, HEAD_SIZE))
        value_rows = jnp.broadcast_to(value_rows, (local_heads, sequence_length, HEAD_SIZE))
    heads = attend(query, key_rows, value_rows, keep_bits)
    heads_out = heads.transpose(1, 0, 2).reshape(sequence_length, query_cols)
    terms = jnp.dot(heads_out, output_weight, preferred_element_type=jnp.float32).astype(
        jnp.bfloat16
    )
    total = lax.psum_scatter(terms, "tensor", scatter_dimension=0, tiled=True).astype(jnp.float32)
    return (inputs + total).astype(jnp.bfloat16)


MESH = pl.DeviceIdType.MESH
PIECES = 4


def chain_kernel(
    n,
    x_ref,
    gain_ref,
    keep_ref,
    cos_ref,
    sin_ref,
    wq_hbm,
    wk_hbm,
    wv_hbm,
    wo_hbm,
    out_ref,
    wq,
    wk,
    wv,
    wo,
    gathered,
    parts,
    incoming,
    keys,
    values,
    queries,
    joined,
    projected,
    load_sem,
    ag_send,
    ag_recv,
    rs_send,
    rs_recv,
):
    me = lax.axis_index("tensor")
    rows, width = x_ref.shape
    length = n * rows
    step = width // PIECES
    heads = wq.shape[1] // HEAD_SIZE
    kv_heads = wk.shape[1] // HEAD_SIZE
    group = heads // kv_heads
    blocks = keep_ref.shape[2]
    has_left = me > 0
    has_right = me < n - 1
    is_lower = me < n // 2
    is_end = jnp.logical_or(me == 0, me == n - 1)

    loads = [
        pltpu.make_async_copy(src, dst, load_sem.at[i])
        for i, (src, dst) in enumerate(
            ((wq_hbm, wq), (wk_hbm, wk), (wv_hbm, wv), (wo_hbm, wo))
        )
    ]

    barrier = pltpu.get_barrier_semaphore()

    @pl.when(has_left)
    def _():
        pl.semaphore_signal(barrier, inc=1, device_id={"tensor": me - 1}, device_id_type=MESH)

    @pl.when(has_right)
    def _():
        pl.semaphore_signal(barrier, inc=1, device_id={"tensor": me + 1}, device_id_type=MESH)

    for load in loads:
        load.start()

    inputs = x_ref[...].astype(jnp.float32)
    scaled = lax.rsqrt(jnp.mean(inputs * inputs, axis=-1, keepdims=True) + 1e-05)
    gathered[me] = (inputs * scaled * gain_ref[...]).astype(jnp.bfloat16)
    keys[...] = jnp.zeros_like(keys)
    values[...] = jnp.zeros_like(values)

    pl.semaphore_wait(barrier, jnp.where(is_end, 1, 2))

    def cols(c):
        return pl.ds(pl.multiple_of(c * step, step), step)

    def gather_copy(way, block, c):
        piece = gathered.at[block, :, cols(c)]
        return pltpu.make_async_remote_copy(
            src_ref=piece,
            dst_ref=piece,
            send_sem=ag_send.at[way, block, c],
            recv_sem=ag_recv.at[block, c],
            device_id={"tensor": me + 1 - 2 * way},
            device_id_type=MESH,
        )

    def sum_copy(way, token, c):
        return pltpu.make_async_remote_copy(
            src_ref=parts.at[token, :, cols(c)],
            dst_ref=incoming.at[way, token, :, cols(c)],
            send_sem=rs_send.at[token, c],
            recv_sem=rs_recv.at[way, token, c],
            device_id={"tensor": me + 1 - 2 * way},
            device_id_type=MESH,
        )

    def each(first, last, body):
        lax.fori_loop(first, last, lambda c, carry: (body(c), carry)[1], 0)

    early = jnp.where(me == 0, PIECES, jnp.minimum(me, PIECES))

    @pl.when(has_right)
    def _():
        each(0, early, lambda c: gather_copy(0, me, c).start())

    @pl.when(has_left)
    def _():
        each(0, PIECES, lambda c: gather_copy(1, me, c).start())

    def phase(p, token, streams):
        @pl.when(jnp.logical_and(p == me, has_right))
        def _():
            each(early, PIECES, lambda c: gather_copy(0, me, c).start())

        from_left = jnp.logical_and(p >= 0, p < me)
        other = me + 1 + p
        from_right = jnp.logical_and(p >= 0, other < n)

        def piece(c):
            @pl.when(from_left)
            def _():
                gather_copy(0, p, c).wait_recv()

                @pl.when(has_right)
                def _():
                    gather_copy(0, p, c).start()

            @pl.when(from_right)
            def _():
                gather_copy(1, other, c).wait_recv()

                @pl.when(has_left)
                def _():
                    gather_copy(1, other, c).start()

            @pl.when(streams)
            def _():
                multiply_piece(token, c)

        @pl.when(streams)
        def _():
            projected[...] = jnp.zeros_like(projected)

        each(0, PIECES, piece)

    def rotated(t, cosine, sine):
        return t * cosine + pltpu.roll(t, HEAD_SIZE // 2, 1) * sine

    def multiply(token, where):
        block = gathered[token, :, where]
        q_cols, kv_cols = wq.shape[1], wk.shape[1]
        return (
            (slice(0, q_cols), jnp.dot(block, wq[where, :], preferred_element_type=jnp.float32)),
            (
                slice(q_cols, q_cols + kv_cols),
                jnp.dot(block, wk[where, :], preferred_element_type=jnp.float32),
            ),
            (
                slice(q_cols + kv_cols, q_cols + 2 * kv_cols),
                jnp.dot(block, wv[where, :], preferred_element_type=jnp.float32),
            ),
        )

    def multiply_whole(token):
        for span, product in multiply(token, slice(None)):
            projected[:, span] = product

    def multiply_piece(token, c):
        for span, product in multiply(token, cols(c)):
            projected[:, span] += product

    def attend_block(token):
        first_row = pl.multiple_of(token * rows, rows)
        where = pl.ds(first_row, rows)
        q_cols, kv_cols = wq.shape[1], wk.shape[1]
        cosine = cos_ref[where, :]
        sine = sin_ref[where, :]
        key_raw = projected[:, q_cols : q_cols + kv_cols].astype(jnp.bfloat16).astype(jnp.float32)
        value = projected[:, q_cols + kv_cols :].astype(jnp.bfloat16)
        for g in range(kv_heads):
            span = slice(g * HEAD_SIZE, (g + 1) * HEAD_SIZE)
            keys[g, where, :] = rotated(key_raw[:, span], cosine, sine).astype(jnp.bfloat16)
            values[g, where, :] = value[:, span]
        for g in range(kv_heads):
            wide = slice(g * group * HEAD_SIZE, (g + 1) * group * HEAD_SIZE)
            raw = projected[:, wide]
            for h in range(group):
                one = raw[:, h * HEAD_SIZE : (h + 1) * HEAD_SIZE]
                queries[g, h * rows : (h + 1) * rows, :] = rotated(one, cosine, sine).astype(
                    jnp.bfloat16
                )
        column = lax.broadcasted_iota(jnp.int32, (rows, length), 1)
        row = lax.broadcasted_iota(jnp.int32, (rows, length), 0) + first_row
        causal = column <= row
        which = lax.broadcasted_iota(jnp.int32, (1, length), 1) // (length // blocks)
        for g in range(kv_heads):
            scores = lax.dot_general(
                queries[g], keys[g], (((1,), (1,)), ((), ())), preferred_element_type=jnp.float32
            ) / np.float32(np.sqrt(np.float32(HEAD_SIZE)))
            dropped = []
            for h in range(group):
                one = jnp.where(causal, scores[h * rows : (h + 1) * rows], jnp.float32(-1e30))
                highest = jnp.max(one, axis=-1, keepdims=True)
                terms = jnp.exp(one - highest)
                inverse = 1.0 / (jnp.sum(terms, axis=-1, keepdims=True) * jnp.float32(0.9))
                keeper = jnp.zeros((1, length), jnp.float32)
                for j in range(blocks):
                    bit = keep_ref[g * group + h, token, j].astype(jnp.float32)
                    keeper = jnp.where(which == j, bit, keeper)
                dropped.append((terms * inverse * keeper).astype(jnp.bfloat16))
            result = jnp.dot(
                jnp.concatenate(dropped, axis=0), values[g], preferred_element_type=jnp.float32
            ).astype(jnp.bfloat16)
            for h in range(group):
                at = (g * group + h) * HEAD_SIZE
                joined[:, at : at + HEAD_SIZE] = result[h * rows : (h + 1) * rows]

    def pass_on(token, c):
        def send(way, receives):
            @pl.when(receives)
            def _():
                sum_copy(way, token, c).wait_recv()
                total = parts[token, :, cols(c)].astype(jnp.float32) + incoming[
                    way, token, :, cols(c)
                ].astype(jnp.float32)
                parts[token, :, cols(c)] = total.astype(jnp.bfloat16)

            sum_copy(way, token, c).start()

        @pl.when(me < token)
        def _():
            send(0, has_left)

        @pl.when(me > token)
        def _():
            send(1, has_right)

    def iteration(i, carry):
        streams = jnp.logical_and(is_end, i != me)

        @pl.when(jnp.logical_and(i == 0, me == n - 1))
        def _():
            for load in loads[:3]:
                load.wait()

        phase(jnp.where(me == 0, i - 1, i), i, streams)

        @pl.when(jnp.logical_and(i == 0, me < n - 1))
        def _():
            for load in loads[:3]:
                load.wait()

        @pl.when(jnp.logical_not(streams))
        def _():
            multiply_whole(i)

        attend_block(i)

        @pl.when(i == 0)
        def _():
            loads[3].wait()

        def project(c):
            parts[i, :, cols(c)] = jnp.dot(
                joined[...], wo[:, cols(c)], preferred_element_type=jnp.float32
            ).astype(jnp.bfloat16)

            @pl.when(is_end)
            def _():
                pass_on(i, c)

        each(0, PIECES, project)

        ready = jnp.where(is_lower, me + 1, 1)

        @pl.when(jnp.logical_and(jnp.logical_not(is_end), i == ready))
        def _():
            each(0, PIECES, lambda c: pass_on(jnp.where(is_lower, me + 1, 0), c))

        return carry

    lax.fori_loop(0, n, iteration, 0)

    @pl.when(jnp.logical_not(is_end))
    def _():
        def both(c):
            pass_on(jnp.where(is_lower, 0, 1), c)
            pass_on(n - 1, c)

        each(0, PIECES, both)

    def finish(c):
        total = x_ref[:, cols(c)].astype(jnp.float32) + parts[me, :, cols(c)].astype(jnp.float32)
        out_ref[:, cols(c)] = total.astype(out_ref.dtype)
        for way, exists in ((0, has_left), (1, has_right)):

            @pl.when(exists)
            def _():
                sum_copy(way, me, c).wait_recv()

        from_left = jnp.where(has_left, incoming[0, me, :, cols(c)].astype(jnp.float32), 0.0)
        from_right = jnp.where(has_right, incoming[1, me, :, cols(c)].astype(jnp.float32), 0.0)
        out_ref[:, cols(c)] = (total + from_left + from_right).astype(out_ref.dtype)

    each(0, PIECES, finish)

    def drain(block, c):
        @pl.when(jnp.logical_and(block <= me, has_right))
        def _():
            gather_copy(0, block, c).wait_send()

        @pl.when(jnp.logical_and(block >= me, has_left))
        def _():
            gather_copy(1, block, c).wait_send()

        @pl.when(block != me)
        def _():
            sum_copy(0, block, c).wait_send()

    each(0, n, lambda block: each(0, PIECES, lambda c: drain(block, c)))


def fused(layer_input, norm_gain, query_weight, key_weight, value_matrix, output_weight, keep_bits):
    n = lax.axis_size("tensor")
    rows, width = layer_input.shape
    length = n * rows
    half = HEAD_SIZE // 2
    freqs = theta_base ** (-(np.arange(half, dtype=np.float64) * 2.0) / HEAD_SIZE)
    angles = np.arange(length)[:, None] * freqs[None, :]
    cosine = np.concatenate([np.cos(angles), np.cos(angles)], axis=1).astype(np.float32)
    sine = np.concatenate([-np.sin(angles), np.sin(angles)], axis=1).astype(np.float32)
    heads = query_weight.shape[1] // HEAD_SIZE
    kv_heads = key_weight.shape[1] // HEAD_SIZE
    vmem = pl.BlockSpec(memory_space=pltpu.VMEM)
    hbm = pl.BlockSpec(memory_space=pltpu.HBM)
    bf16 = jnp.bfloat16
    weights = (query_weight, key_weight, value_matrix, output_weight)
    return pl.pallas_call(
        functools.partial(chain_kernel, n),
        out_shape=jax.ShapeDtypeStruct((rows, width), bf16),
        in_specs=[vmem, vmem, pl.BlockSpec(memory_space=pltpu.SMEM), vmem, vmem] + [hbm] * 4,
        out_specs=vmem,
        scratch_shapes=[pltpu.VMEM(w.shape, bf16) for w in weights]
        + [
            pltpu.VMEM((n, rows, width), bf16),
            pltpu.VMEM((n, rows, width), bf16),
            pltpu.VMEM((2, n, rows, width), bf16),
            pltpu.VMEM((kv_heads, length, HEAD_SIZE), bf16),
            pltpu.VMEM((kv_heads, length, HEAD_SIZE), bf16),
            pltpu.VMEM((kv_heads, heads // kv_heads * rows, HEAD_SIZE), bf16),
            pltpu.VMEM((rows, heads * HEAD_SIZE), bf16),
            pltpu.VMEM((rows, (heads + 2 * kv_heads) * HEAD_SIZE), jnp.float32),
            pltpu.SemaphoreType.DMA((4,)),
            pltpu.SemaphoreType.DMA((2, n, PIECES)),
            pltpu.SemaphoreType.DMA((n, PIECES)),
            pltpu.SemaphoreType.DMA((n, PIECES)),
            pltpu.SemaphoreType.DMA((2, n, PIECES)),
        ],
        compiler_params=pltpu.CompilerParams(
            collective_id=0, has_side_effects=True, vmem_limit_bytes=60 * 2**20
        ),
    )(layer_input, norm_gain[None, :], keep_bits, cosine, sine, *weights)


def solution(mesh):
    in_specs = (
        P(("dp", "tensor"), None),
        P(),
        P(None, "tensor"),
        P(None, "tensor"),
        P(None, "tensor"),
        P("tensor", None),
        P(("dp", "tensor"), None, None),
    )
    out_specs = P(("dp", "tensor"), None)
    return jax.shard_map(
        on_device, mesh=mesh, in_specs=in_specs, out_specs=out_specs, check_vma=False
    )
```

profile of v0, /device:TPU:28, one launch (start us, length us, event | category | flops | bytes accessed | tf_op | source)
XLA Modules:
  0.0 69.7 jit_solution(3109073882216970734)
XLA Ops:
  0.0 1.4 %copy.10.keep_ref = s32[8,4,4]{2,1,0:T(4,128)} copy(s32[8,4,4]{0,2,1:T(4,128)} %param.15) | data formatting | bytes 1024 | tf_op args[6]
  1.4 66.4 %shard_map.91 = bf16[64,4096]{1,0:T(8,128)(2,1)} custom-call(bf16[64,4096]{1,0:T(8,128)(2,1)} %x_ref.1, f32[1,4096]{1,0:T(1,128)} %bitcast.1, s32[8,4,4]{2,1,0:T(4,128)} %copy.10.keep_ref, f32[256,128]{1,0:T(8,128)} %constant.4.clone.cos_ref, f32[256,128]{1,0:T(8,128)} %constant.5.clone.sin_ref, bf16[4096,1024]{1,0:T(8,128)(2,1)} %wq_hbm.1, ...), custom_call_target="tpu_custom_call" | custom-call | tf_op jit(solution)/shard_map/pallas_call | solution.py:499
  67.8 1.9 %copy.12 = bf16[64,4096]{1,0:T(8,128)(2,1)} copy(bf16[64,4096]{1,0:T(8,128)(2,1)} %shard_map.91) | data formatting | bytes 1048576
where the time goes:
time: 69.9 us; the launch traced here: 69.7 us
  Pallas kernels  66.4 us (95%)
  local copies, waits for them, and re-layouts  3.26 us (5%)
    pallas_call x1, Pallas kernels, fused(): pl.pallas_call(functools.partial(chain_kernel, n), out_shape=jax.ShapeDty...  66.4 us
    unnamed x2, local copies, waits for them, and re-layouts  3.26 us

commit v1 on v0

--- a/solution.py
+++ b/solution.py
@@ -90,7 +90,8 @@
     layer_input, norm_gain, query_weight, key_weight, value_matrix, output_weight, keep_bits
 ):
     devices = lax.axis_size("tensor")
-    if 1 < devices <= KEY_VALUE_HEADS // 2 and layer_input.shape[0] == BLOCK:
+    paired = lax.axis_size("dp") % 2 == 0
+    if devices == CHAIN and paired and layer_input.shape[0] == BLOCK:
         return fused(
             layer_input,
             norm_gain,
@@ -157,21 +158,29 @@
 
 
 MESH = pl.DeviceIdType.MESH
-PIECES = 4
+CHAIN = 4
+PIECES = 8
+SLOT = 4
+LAG = 4
 
 
 def chain_kernel(
     n,
+    x_hbm,
+    gain_hbm,
+    keep_hbm,
+    cos_hbm,
+    sin_hbm,
+    wq_hbm,
+    wk_hbm,
+    wv_hbm,
+    wo_hbm,
+    out_ref,
     x_ref,
     gain_ref,
     keep_ref,
     cos_ref,
     sin_ref,
-    wq_hbm,
-    wk_hbm,
-    wv_hbm,
-    wo_hbm,
-    out_ref,
     wq,
     wk,
     wv,
@@ -189,6 +198,7 @@
     ag_recv,
     rs_send,
     rs_recv,
+    turn,
 ):
     me = lax.axis_index("tensor")
     rows, width = x_ref.shape
@@ -197,16 +207,29 @@
     heads = wq.shape[1] // HEAD_SIZE
     kv_heads = wk.shape[1] // HEAD_SIZE
     group = heads // kv_heads
-    blocks = keep_ref.shape[2]
+    blocks = keep_ref.shape[1]
     has_left = me > 0
     has_right = me < n - 1
     is_lower = me < n // 2
     is_end = jnp.logical_or(me == 0, me == n - 1)
+    pair = lax.axis_index("dp")
+    leads = lax.rem(pair, 2) == 0
+    partner = jnp.where(leads, pair + 1, pair - 1)
 
     loads = [
         pltpu.make_async_copy(src, dst, load_sem.at[i])
         for i, (src, dst) in enumerate(
-            ((wq_hbm, wq), (wk_hbm, wk), (wv_hbm, wv), (wo_hbm, wo))
+            (
+                (x_hbm, x_ref),
+                (gain_hbm, gain_ref),
+                (keep_hbm, keep_ref),
+                (wk_hbm, wk),
+                (wv_hbm, wv),
+                (wq_hbm, wq),
+                (cos_hbm, cos_ref),
+                (sin_hbm, sin_ref),
+                (wo_hbm, wo),
+            )
         )
     ]
 
@@ -220,131 +243,143 @@
     def _():
         pl.semaphore_signal(barrier, inc=1, device_id={"tensor": me + 1}, device_id_type=MESH)
 
-    for load in loads:
+    pl.semaphore_signal(barrier, inc=1, device_id={"dp": partner}, device_id_type=MESH)
+
+    for load in loads[:3]:
         load.start()
+    loads[0].wait()
+    loads[1].wait()
+    for load in loads[3:]:
+        load.start()
+
+    def slot(device, block):
+        return lax.rem(block + jnp.where(device == 2, 2, 0), n)
 
     inputs = x_ref[...].astype(jnp.float32)
     scaled = lax.rsqrt(jnp.mean(inputs * inputs, axis=-1, keepdims=True) + 1e-05)
-    gathered[me] = (inputs * scaled * gain_ref[...]).astype(jnp.bfloat16)
-    keys[...] = jnp.zeros_like(keys)
-    values[...] = jnp.zeros_like(values)
-
-    pl.semaphore_wait(barrier, jnp.where(is_end, 1, 2))
+    gathered[slot(me, me)] = (inputs * scaled * gain_ref[...]).astype(jnp.bfloat16)
+
+    pl.semaphore_wait(barrier, jnp.where(is_end, 2, 3))
 
     def cols(c):
         return pl.ds(pl.multiple_of(c * step, step), step)
 
     def gather_copy(way, block, c):
-        piece = gathered.at[block, :, cols(c)]
+        to = me + 1 - 2 * way
         return pltpu.make_async_remote_copy(
+            src_ref=gathered.at[slot(me, block), :, cols(c)],
+            dst_ref=gathered.at[slot(to, block), :, cols(c)],
+            send_sem=ag_send.at[way, block],
+            recv_sem=ag_recv.at[block, c],
+            device_id={"tensor": to},
+            device_id_type=MESH,
+        )
+
+    def arrived(block, c):
+        arrival(block, c)
+
+    def arrival(block, c):
+        piece = gathered.at[slot(me, block), :, cols(c)]
+        pltpu.make_async_remote_copy(
             src_ref=piece,
             dst_ref=piece,
-            send_sem=ag_send.at[way, block, c],
+            send_sem=ag_send.at[0, 0],
             recv_sem=ag_recv.at[block, c],
-            device_id={"tensor": me + 1 - 2 * way},
+            device_id={"tensor": jnp.where(has_right, me + 1, me - 1)},
             device_id_type=MESH,
-        )
+        ).wait_recv()
 
     def sum_copy(way, token, c):
         return pltpu.make_async_remote_copy(
             src_ref=parts.at[token, :, cols(c)],
             dst_ref=incoming.at[way, token, :, cols(c)],
-            send_sem=rs_send.at[token, c],
+            send_sem=rs_send.at[token],
             recv_sem=rs_recv.at[way, token, c],
             device_id={"tensor": me + 1 - 2 * way},
             device_id_type=MESH,
         )
 
+    def whole_copy(buffer, sem, index):
+        return pltpu.make_async_remote_copy(
+            src_ref=buffer.at[index],
+            dst_ref=buffer.at[index],
+            send_sem=sem,
+            recv_sem=ag_recv.at[0, 0],
+            device_id={"tensor": jnp.where(has_right, me + 1, me - 1)},
+            device_id_type=MESH,
+        )
+
     def each(first, last, body):
         lax.fori_loop(first, last, lambda c, carry: (body(c), carry)[1], 0)
 
-    early = jnp.where(me == 0, PIECES, jnp.minimum(me, PIECES))
-
-    @pl.when(has_right)
-    def _():
-        each(0, early, lambda c: gather_copy(0, me, c).start())
-
-    @pl.when(has_left)
-    def _():
-        each(0, PIECES, lambda c: gather_copy(1, me, c).start())
-
-    def phase(p, token, streams):
-        @pl.when(jnp.logical_and(p == me, has_right))
-        def _():
-            each(early, PIECES, lambda c: gather_copy(0, me, c).start())
-
-        from_left = jnp.logical_and(p >= 0, p < me)
-        other = me + 1 + p
-        from_right = jnp.logical_and(p >= 0, other < n)
-
-        def piece(c):
-            @pl.when(from_left)
-            def _():
-                gather_copy(0, p, c).wait_recv()
-
-                @pl.when(has_right)
-                def _():
-                    gather_copy(0, p, c).start()
-
-            @pl.when(from_right)
-            def _():
-                gather_copy(1, other, c).wait_recv()
-
-                @pl.when(has_left)
-                def _():
-                    gather_copy(1, other, c).start()
-
-            @pl.when(streams)
-            def _():
-                multiply_piece(token, c)
-
-        @pl.when(streams)
-        def _():
-            projected[...] = jnp.zeros_like(projected)
-
-        each(0, PIECES, piece)
+    early = jnp.where(me == 0, PIECES, jnp.where(leads, me * PIECES // 2, 0))
+
+    def send_own():
+        @pl.when(has_right)
+        def _():
+            each(0, early, lambda c: gather_copy(0, me, c).start())
+
+        @pl.when(has_left)
+        def _():
+            each(0, PIECES, lambda c: gather_copy(1, me, c).start())
+
+    pl.when(leads)(send_own)
+
+    def take_turn():
+        @pl.when(jnp.logical_not(leads))
+        def _():
+            pl.semaphore_wait(turn, 1)
+            send_own()
+
+    def give_turn():
+        pl.semaphore_signal(turn, inc=1, device_id={"dp": partner}, device_id_type=MESH)
+
+    def rest_of_own():
+        each(early, PIECES, lambda c: gather_copy(0, me, c).start())
+
+    def forward(way, block, c):
+        arrived(block, c)
+        gather_copy(way, block, c).start()
 
     def rotated(t, cosine, sine):
         return t * cosine + pltpu.roll(t, HEAD_SIZE // 2, 1) * sine
 
-    def multiply(token, where):
-        block = gathered[token, :, where]
-        q_cols, kv_cols = wq.shape[1], wk.shape[1]
-        return (
-            (slice(0, q_cols), jnp.dot(block, wq[where, :], preferred_element_type=jnp.float32)),
-            (
-                slice(q_cols, q_cols + kv_cols),
-                jnp.dot(block, wk[where, :], preferred_element_type=jnp.float32),
-            ),
-            (
-                slice(q_cols + kv_cols, q_cols + 2 * kv_cols),
-                jnp.dot(block, wv[where, :], preferred_element_type=jnp.float32),
-            ),
-        )
-
-    def multiply_whole(token):
-        for span, product in multiply(token, slice(None)):
-            projected[:, span] = product
-
-    def multiply_piece(token, c):
-        for span, product in multiply(token, cols(c)):
-            projected[:, span] += product
+    def multiply(first, count, where):
+        block = gathered[pl.ds(first, count), :, where].reshape(count * rows, -1)
+        spans = []
+        at = 0
+        for weight in (wq, wk, wv):
+            product = jnp.dot(block, weight[where, :], preferred_element_type=jnp.float32)
+            spans.append((slice(at, at + weight.shape[1]), product.reshape(count, rows, -1)))
+            at += weight.shape[1]
+        return spans
+
+    def multiply_whole(first):
+        for span, product in multiply(first, 1, slice(None)):
+            projected[pl.ds(first, 1), :, span] = product
+
+    def multiply_piece(first, count, c):
+        for span, product in multiply(first, count, cols(c)):
+            projected[pl.ds(first, count), :, span] += product
 
     def attend_block(token):
+        here = slot(me, token)
         first_row = pl.multiple_of(token * rows, rows)
         where = pl.ds(first_row, rows)
         q_cols, kv_cols = wq.shape[1], wk.shape[1]
         cosine = cos_ref[where, :]
         sine = sin_ref[where, :]
-        key_raw = projected[:, q_cols : q_cols + kv_cols].astype(jnp.bfloat16).astype(jnp.float32)
-        value = projected[:, q_cols + kv_cols :].astype(jnp.bfloat16)
+        key_raw = (
+            projected[here, :, q_cols : q_cols + kv_cols].astype(jnp.bfloat16).astype(jnp.float32)
+        )
+        value = projected[here, :, q_cols + kv_cols :].astype(jnp.bfloat16)
         for g in range(kv_heads):
             span = slice(g * HEAD_SIZE, (g + 1) * HEAD_SIZE)
             keys[g, where, :] = rotated(key_raw[:, span], cosine, sine).astype(jnp.bfloat16)
             values[g, where, :] = value[:, span]
         for g in range(kv_heads):
             wide = slice(g * group * HEAD_SIZE, (g + 1) * group * HEAD_SIZE)
-            raw = projected[:, wide]
+            raw = projected[here, :, wide]
             for h in range(group):
                 one = raw[:, h * HEAD_SIZE : (h + 1) * HEAD_SIZE]
                 queries[g, h * rows : (h + 1) * rows, :] = rotated(one, cosine, sine).astype(
@@ -357,7 +392,7 @@
         for g in range(kv_heads):
             scores = lax.dot_general(
                 queries[g], keys[g], (((1,), (1,)), ((), ())), preferred_element_type=jnp.float32
-            ) / np.float32(np.sqrt(np.float32(HEAD_SIZE)))
+            ) * np.float32(1.0 / np.sqrt(HEAD_SIZE))
             dropped = []
             for h in range(group):
                 one = jnp.where(causal, scores[h * rows : (h + 1) * rows], jnp.float32(-1e30))
@@ -366,7 +401,7 @@
                 inverse = 1.0 / (jnp.sum(terms, axis=-1, keepdims=True) * jnp.float32(0.9))
                 keeper = jnp.zeros((1, length), jnp.float32)
                 for j in range(blocks):
-                    bit = keep_ref[g * group + h, token, j].astype(jnp.float32)
+                    bit = keep_ref[token, j, g * group + h].astype(jnp.float32)
                     keeper = jnp.where(which == j, bit, keeper)
                 dropped.append((terms * inverse * keeper).astype(jnp.bfloat16))
             result = jnp.dot(
@@ -374,111 +409,215 @@
             ).astype(jnp.bfloat16)
             for h in range(group):
                 at = (g * group + h) * HEAD_SIZE
-                joined[:, at : at + HEAD_SIZE] = result[h * rows : (h + 1) * rows]
+                joined[token, :, at : at + HEAD_SIZE] = result[h * rows : (h + 1) * rows]
+
+    def project(first, count, c):
+        mixed = joined[pl.ds(first, count)].reshape(count * rows, -1)
+        parts[pl.ds(first, count), :, cols(c)] = (
+            jnp.dot(mixed, wo[:, cols(c)], preferred_element_type=jnp.float32)
+            .astype(jnp.bfloat16)
+            .reshape(count, rows, -1)
+        )
 
     def pass_on(token, c):
-        def send(way, receives):
-            @pl.when(receives)
+        way = jnp.where(me < token, 0, 1)
+        sum_copy(way, token, c).wait_recv()
+        total = parts[token, :, cols(c)].astype(jnp.float32) + incoming[
+            way, token, :, cols(c)
+        ].astype(jnp.float32)
+        parts[token, :, cols(c)] = total.astype(jnp.bfloat16)
+        sum_copy(way, token, c).start()
+
+    keys[...] = jnp.zeros_like(keys)
+    values[...] = jnp.zeros_like(values)
+    projected[...] = jnp.zeros_like(projected)
+    for load in loads[3:6]:
+        load.wait()
+
+    def wait_tables():
+        for load in loads[6:] + loads[2:3]:
+            load.wait()
+
+    def drain_gather(early_up, early_down):
+        def drain(block):
+            @pl.when(functools.reduce(jnp.logical_and, (block <= me, has_right, block >= early_up)))
             def _():
-                sum_copy(way, token, c).wait_recv()
-                total = parts[token, :, cols(c)].astype(jnp.float32) + incoming[
-                    way, token, :, cols(c)
-                ].astype(jnp.float32)
-                parts[token, :, cols(c)] = total.astype(jnp.bfloat16)
-
-            sum_copy(way, token, c).start()
-
-        @pl.when(me < token)
-        def _():
-            send(0, has_left)
-
-        @pl.when(me > token)
-        def _():
-            send(1, has_right)
-
-    def iteration(i, carry):
-        streams = jnp.logical_and(is_end, i != me)
-
-        @pl.when(jnp.logical_and(i == 0, me == n - 1))
-        def _():
-            for load in loads[:3]:
-                load.wait()
-
-        phase(jnp.where(me == 0, i - 1, i), i, streams)
-
-        @pl.when(jnp.logical_and(i == 0, me < n - 1))
-        def _():
-            for load in loads[:3]:
-                load.wait()
-
-        @pl.when(jnp.logical_not(streams))
-        def _():
-            multiply_whole(i)
-
-        attend_block(i)
-
-        @pl.when(i == 0)
-        def _():
-            loads[3].wait()
-
-        def project(c):
-            parts[i, :, cols(c)] = jnp.dot(
-                joined[...], wo[:, cols(c)], preferred_element_type=jnp.float32
-            ).astype(jnp.bfloat16)
-
-            @pl.when(is_end)
+                sent(0, block)
+
+            @pl.when(functools.reduce(jnp.logical_and, (block >= me, has_left, block >= early_down)))
             def _():
-                pass_on(i, c)
-
-        each(0, PIECES, project)
-
-        ready = jnp.where(is_lower, me + 1, 1)
-
-        @pl.when(jnp.logical_and(jnp.logical_not(is_end), i == ready))
-        def _():
-            each(0, PIECES, lambda c: pass_on(jnp.where(is_lower, me + 1, 0), c))
-
-        return carry
-
-    lax.fori_loop(0, n, iteration, 0)
+                sent(1, block)
+
+        each(0, n, drain)
+
+    def sent(way, block):
+        whole_copy(gathered, ag_send.at[way, block], block).wait_send()
+
+    @pl.when(is_end)
+    def _():
+        way = jnp.where(me == 0, 0, 1)
+        multiply_whole(me)
+        wait_tables()
+
+        @pl.when(jnp.logical_and(leads, me > 0))
+        def _():
+            sent(1, me)
+            give_turn()
+
+        take_turn()
+
+        def iteration(i, carry):
+            @pl.when(i != me)
+            def _():
+                def piece(c):
+                    arrived(i, c)
+                    multiply_piece(i, 1, c)
+
+                each(0, PIECES, piece)
+
+            attend_block(i)
+
+            @pl.when(functools.reduce(jnp.logical_and, (i == 0, me == 0, leads)))
+            def _():
+                sent(0, 0)
+                give_turn()
+
+            def out_piece(c):
+                project(i, 1, c)
+
+                @pl.when(i != me)
+                def _():
+                    sum_copy(way, i, c).start()
+
+            each(0, PIECES, out_piece)
+            return carry
+
+        lax.fori_loop(0, n, iteration, 0)
+
+        drain_gather(jnp.where(leads, n, 0), jnp.where(leads, n, 0))
+
+        def finish(c):
+            sum_copy(1 - way, me, c).wait_recv()
+            out_ref[:, cols(c)] = (
+                x_ref[:, cols(c)].astype(jnp.float32)
+                + parts[me, :, cols(c)].astype(jnp.float32)
+                + incoming[1 - way, me, :, cols(c)].astype(jnp.float32)
+            ).astype(out_ref.dtype)
+
+        each(0, PIECES, finish)
 
     @pl.when(jnp.logical_not(is_end))
     def _():
+        last = jnp.where(is_lower, n - 1, 1)
+        last_way = jnp.where(is_lower, 1, 0)
+        skew = (me - 1) * 2
+        split = jnp.where(is_lower, n - 1, 1)
+        take_turn()
+
+        def multiply_last(c):
+            multiply_piece(3, 1, c)
+
+        def attend(i):
+            attend_block(i)
+
         def both(c):
-            pass_on(jnp.where(is_lower, 0, 1), c)
-            pass_on(n - 1, c)
-
-        each(0, PIECES, both)
-
-    def finish(c):
-        total = x_ref[:, cols(c)].astype(jnp.float32) + parts[me, :, cols(c)].astype(jnp.float32)
-        out_ref[:, cols(c)] = total.astype(out_ref.dtype)
-        for way, exists in ((0, has_left), (1, has_right)):
-
-            @pl.when(exists)
+            @pl.when(c < PIECES)
             def _():
+                forward(1, me + 1, c)
+
+            @pl.when(c >= skew)
+            def _():
+                forward(0, 0, c - skew)
+                multiply_piece(0, 3, c - skew)
+
+        each(0, PIECES + skew, both)
+        wait_tables()
+
+        @pl.when(is_lower)
+        def _():
+            rest_of_own()
+
+        @pl.when(leads)
+        def _():
+            sent(1, me)
+            sent(1, me + 1)
+            give_turn()
+
+        each(0, split, attend)
+
+        @pl.when(is_lower)
+        def _():
+            def out_piece(c):
+                project(0, 3, c)
+                forward(last_way, last, c)
+
+            each(0, PIECES, out_piece)
+
+        @pl.when(jnp.logical_not(is_lower))
+        def _():
+            def out_piece(c):
+                project(0, 1, c)
+                forward(last_way, last, c)
+
+            each(0, PIECES, out_piece)
+            rest_of_own()
+
+        each(0, PIECES, lambda c: multiply_last(c))
+        each(split, n, attend)
+
+        @pl.when(is_lower)
+        def _():
+            each(0, PIECES, lambda c: project(n - 1, 1, c))
+
+            def stream(k):
+                token = 2 + k // PIECES
+                pass_on(token, lax.rem(k, PIECES))
+
+                @pl.when(jnp.logical_and(k >= LAG, k < PIECES + LAG))
+                def _():
+                    pass_on(0, k - LAG)
+
+            each(0, 2 * PIECES, stream)
+
+        @pl.when(jnp.logical_not(is_lower))
+        def _():
+            def out_piece(c):
+                project(1, 3, c)
+                pass_on(0, c)
+
+            each(0, PIECES, out_piece)
+
+            def two(c):
+                @pl.when(c < PIECES)
+                def _():
+                    pass_on(1, c)
+
+                @pl.when(c >= LAG)
+                def _():
+                    pass_on(n - 1, c - LAG)
+
+            each(0, PIECES + LAG, two)
+
+        drain_gather(0, jnp.where(leads, me + 2, 0))
+
+        def finish(c):
+            for way in range(2):
                 sum_copy(way, me, c).wait_recv()
-
-        from_left = jnp.where(has_left, incoming[0, me, :, cols(c)].astype(jnp.float32), 0.0)
-        from_right = jnp.where(has_right, incoming[1, me, :, cols(c)].astype(jnp.float32), 0.0)
-        out_ref[:, cols(c)] = (total + from_left + from_right).astype(out_ref.dtype)
-
-    each(0, PIECES, finish)
-
-    def drain(block, c):
-        @pl.when(jnp.logical_and(block <= me, has_right))
-        def _():
-            gather_copy(0, block, c).wait_send()
-
-        @pl.when(jnp.logical_and(block >= me, has_left))
-        def _():
-            gather_copy(1, block, c).wait_send()
-
-        @pl.when(block != me)
-        def _():
-            sum_copy(0, block, c).wait_send()
-
-    each(0, n, lambda block: each(0, PIECES, lambda c: drain(block, c)))
+            out_ref[:, cols(c)] = (
+                x_ref[:, cols(c)].astype(jnp.float32)
+                + parts[me, :, cols(c)].astype(jnp.float32)
+                + incoming[0, me, :, cols(c)].astype(jnp.float32)
+                + incoming[1, me, :, cols(c)].astype(jnp.float32)
+            ).astype(out_ref.dtype)
+
+        each(0, PIECES, finish)
+
+    def drain(token):
+        @pl.when(token != me)
+        def _():
+            whole_copy(parts, rs_send.at[token], token).wait_send()
+
+    each(0, n, drain)
 
 
 def fused(layer_input, norm_gain, query_weight, key_weight, value_matrix, output_weight, keep_bits):
@@ -499,9 +638,16 @@
     return pl.pallas_call(
         functools.partial(chain_kernel, n),
         out_shape=jax.ShapeDtypeStruct((rows, width), bf16),
-        in_specs=[vmem, vmem, pl.BlockSpec(memory_space=pltpu.SMEM), vmem, vmem] + [hbm] * 4,
+        in_specs=[hbm] * 9,
         out_specs=vmem,
-        scratch_shapes=[pltpu.VMEM(w.shape, bf16) for w in weights]
+        scratch_shapes=[
+            pltpu.VMEM((rows, width), bf16),
+            pltpu.VMEM((1, width), jnp.float32),
+            pltpu.SMEM(keep_bits.shape[1:] + keep_bits.shape[:1], jnp.int32),
+            pltpu.VMEM(cosine.shape, jnp.float32),
+            pltpu.VMEM(sine.shape, jnp.float32),
+        ]
+        + [pltpu.VMEM(w.shape, bf16) for w in weights]
         + [
             pltpu.VMEM((n, rows, width), bf16),
             pltpu.VMEM((n, rows, width), bf16),
@@ -509,18 +655,19 @@
             pltpu.VMEM((kv_heads, length, HEAD_SIZE), bf16),
             pltpu.VMEM((kv_heads, length, HEAD_SIZE), bf16),
             pltpu.VMEM((kv_heads, heads // kv_heads * rows, HEAD_SIZE), bf16),
-            pltpu.VMEM((rows, heads * HEAD_SIZE), bf16),
-            pltpu.VMEM((rows, (heads + 2 * kv_heads) * HEAD_SIZE), jnp.float32),
-            pltpu.SemaphoreType.DMA((4,)),
+            pltpu.VMEM((n, rows, heads * HEAD_SIZE), bf16),
+            pltpu.VMEM((n, rows, (heads + 2 * kv_heads) * HEAD_SIZE), jnp.float32),
+            pltpu.SemaphoreType.DMA((9,)),
+            pltpu.SemaphoreType.DMA((2, n)),
+            pltpu.SemaphoreType.DMA((n, PIECES)),
+            pltpu.SemaphoreType.DMA((n,)),
             pltpu.SemaphoreType.DMA((2, n, PIECES)),
-            pltpu.SemaphoreType.DMA((n, PIECES)),
-            pltpu.SemaphoreType.DMA((n, PIECES)),
-            pltpu.SemaphoreType.DMA((2, n, PIECES)),
+            pltpu.SemaphoreType.REGULAR,
         ],
         compiler_params=pltpu.CompilerParams(
             collective_id=0, has_side_effects=True, vmem_limit_bytes=60 * 2**20
         ),
-    )(layer_input, norm_gain[None, :], keep_bits, cosine, sine, *weights)
+    )(layer_input, norm_gain[None, :], keep_bits.transpose(1, 2, 0), cosine, sine, *weights)
 
 
 def solution(mesh):

time: 69.9 us -> 62.1 us (0.89)
  the two profiles are of different devices: /device:TPU:28 before, /device:TPU:21 now
where the time goes in v1:
time: 62.1 us; the launch traced here: 61.9 us
  Pallas kernels  60 us (97%)
  local copies, waits for them, and re-layouts  1.87 us (3%)
    pallas_call x1, Pallas kernels, fused(): pl.pallas_call(functools.partial(chain_kernel, n), out_shape=jax.ShapeDty...  60 us
    unnamed x1, local copies, waits for them, and re-layouts  1.87 us

profile of v1, /device:TPU:21, one launch (start us, length us, event | category | flops | bytes accessed | tf_op | source)
XLA Modules:
  0.0 61.9 jit_solution(8839404249548802887)
XLA Ops:
  0.0 60.0 %shard_map.91 = bf16[64,4096]{1,0:T(8,128)(2,1)} custom-call(bf16[64,4096]{1,0:T(8,128)(2,1)} %x_hbm.1, f32[1,4096]{1,0:T(1,128)} %bitcast.2, s32[4,4,8]{2,1,0:T(4,128)} %bitcast.3, f32[256,128]{1,0:T(8,128)} %constant.4.clone.cos_hbm, f32[256,128]{1,0:T(8,128)} %constant.5.clone.sin_hbm, bf16[4096,1024]{1,0:T(8,128)(2,1)} %wq_hbm.1, ...), custom_call_target="tpu_custom_call" | custom-call | tf_op jit(solution)/shard_map/pallas_call | solution.py:638
  60.1 1.9 %copy.11 = bf16[64,4096]{1,0:T(8,128)(2,1)} copy(bf16[64,4096]{1,0:T(8,128)(2,1)} %shard_map.91) | data formatting | bytes 1048576

commit v2 on v1

--- a/solution.py
+++ b/solution.py
@@ -162,6 +162,7 @@
 PIECES = 8
 SLOT = 4
 LAG = 4
+LATE = 16
 
 
 def chain_kernel(
@@ -264,6 +265,9 @@
     def cols(c):
         return pl.ds(pl.multiple_of(c * step, step), step)
 
+    def pairs(k):
+        return pl.ds(pl.multiple_of(k * 2 * step, 2 * step), 2 * step)
+
     def gather_copy(way, block, c):
         to = me + 1 - 2 * way
         return pltpu.make_async_remote_copy(
@@ -358,8 +362,8 @@
         for span, product in multiply(first, 1, slice(None)):
             projected[pl.ds(first, 1), :, span] = product
 
-    def multiply_piece(first, count, c):
-        for span, product in multiply(first, count, cols(c)):
+    def multiply_piece(first, count, where):
+        for span, product in multiply(first, count, where):
             projected[pl.ds(first, count), :, span] += product
 
     def attend_block(token):
@@ -411,10 +415,10 @@
                 at = (g * group + h) * HEAD_SIZE
                 joined[token, :, at : at + HEAD_SIZE] = result[h * rows : (h + 1) * rows]
 
-    def project(first, count, c):
+    def project(first, count, where):
         mixed = joined[pl.ds(first, count)].reshape(count * rows, -1)
-        parts[pl.ds(first, count), :, cols(c)] = (
-            jnp.dot(mixed, wo[:, cols(c)], preferred_element_type=jnp.float32)
+        parts[pl.ds(first, count), :, where] = (
+            jnp.dot(mixed, wo[:, where], preferred_element_type=jnp.float32)
             .astype(jnp.bfloat16)
             .reshape(count, rows, -1)
         )
@@ -465,15 +469,24 @@
             give_turn()
 
         take_turn()
+        ahead = jnp.where(jnp.logical_and(leads, me > 0), n - 2, -1)
+
+        def stream(i):
+            def piece(k):
+                arrived(i, 2 * k)
+                arrived(i, 2 * k + 1)
+                multiply_piece(i, 1, pairs(k))
+
+            each(0, PIECES // 2, piece)
+
+        @pl.when(ahead >= 0)
+        def _():
+            stream(ahead)
 
         def iteration(i, carry):
-            @pl.when(i != me)
-            def _():
-                def piece(c):
-                    arrived(i, c)
-                    multiply_piece(i, 1, c)
-
-                each(0, PIECES, piece)
+            @pl.when(jnp.logical_and(i != me, i != ahead))
+            def _():
+                stream(i)
 
             attend_block(i)
 
@@ -482,18 +495,23 @@
                 sent(0, 0)
                 give_turn()
 
-            def out_piece(c):
-                project(i, 1, c)
-
-                @pl.when(i != me)
-                def _():
-                    sum_copy(way, i, c).start()
-
-            each(0, PIECES, out_piece)
+            def out_piece(k):
+                project(i, 1, pairs(k))
+                sum_copy(way, i, 2 * k).start()
+                sum_copy(way, i, 2 * k + 1).start()
+
+            @pl.when(i != me)
+            def _():
+                each(0, PIECES // 2, out_piece)
+
             return carry
 
         lax.fori_loop(0, n, iteration, 0)
 
+        def out_own(k):
+            project(me, 1, pairs(k))
+
+        each(0, PIECES // 2, out_own)
         drain_gather(jnp.where(leads, n, 0), jnp.where(leads, n, 0))
 
         def finish(c):
@@ -510,64 +528,108 @@
     def _():
         last = jnp.where(is_lower, n - 1, 1)
         last_way = jnp.where(is_lower, 1, 0)
-        skew = (me - 1) * 2
+        skew = jnp.where(leads, (me - 1) * 2, 0)
         split = jnp.where(is_lower, n - 1, 1)
-        take_turn()
-
-        def multiply_last(c):
-            multiply_piece(3, 1, c)
+        share = PIECES // SLOT
+        follows = jnp.logical_not(leads)
 
         def attend(i):
             attend_block(i)
 
-        def both(c):
-            @pl.when(c < PIECES)
-            def _():
-                forward(1, me + 1, c)
-
-            @pl.when(c >= skew)
-            def _():
-                forward(0, 0, c - skew)
-                multiply_piece(0, 3, c - skew)
-
-        each(0, PIECES + skew, both)
+        def multiply_three(c):
+            multiply_piece(0, 3, cols(c))
+
+        @pl.when(leads)
+        def _():
+            def both(c):
+                @pl.when(c < PIECES)
+                def _():
+                    forward(1, me + 1, c)
+
+                @pl.when(jnp.logical_and(c == PIECES // 2, me > 1))
+                def _():
+                    sent(1, me)
+                    give_turn()
+
+                @pl.when(c >= skew)
+                def _():
+                    forward(0, 0, c - skew)
+                    multiply_three(c - skew)
+
+            each(0, PIECES + skew, both)
+
+        @pl.when(follows)
+        def _():
+            take_turn()
+            way = jnp.where(is_lower, 0, 1)
+            first = jnp.where(is_lower, 0, n - 1)
+            second = jnp.where(is_lower, 2, 0)
+            each(0, PIECES, lambda c: forward(way, first, c))
+
+            @pl.when(me > 1)
+            def _():
+                pl.semaphore_wait(turn, 1)
+
+            def then(c):
+                forward(1 - way, second, c)
+                multiply_three(c)
+
+            each(0, PIECES, then)
+
         wait_tables()
 
         @pl.when(is_lower)
         def _():
             rest_of_own()
 
-        @pl.when(leads)
-        def _():
-            sent(1, me)
-            sent(1, me + 1)
-            give_turn()
-
-        each(0, split, attend)
-
-        @pl.when(is_lower)
-        def _():
+            def attend_forward(i):
+                attend(i)
+                each(i * share, (i + 1) * share, lambda c: forward(1, n - 1, c))
+
+                @pl.when(jnp.logical_and(i == 1, leads))
+                def _():
+                    for block in range(2):
+                        sent(0, block)
+                        sent(1, block + 1)
+                    give_turn()
+
+            each(0, n - 1, attend_forward)
+
             def out_piece(c):
-                project(0, 3, c)
-                forward(last_way, last, c)
+                project(0, 3, cols(c))
+
+                @pl.when(c < PIECES - (n - 1) * share)
+                def _():
+                    forward(1, n - 1, c + (n - 1) * share)
 
             each(0, PIECES, out_piece)
 
         @pl.when(jnp.logical_not(is_lower))
         def _():
+            attend(0)
+
             def out_piece(c):
-                project(0, 1, c)
-                forward(last_way, last, c)
+                project(0, 1, cols(c))
+                forward(0, 1, c)
 
             each(0, PIECES, out_piece)
             rest_of_own()
 
-        each(0, PIECES, lambda c: multiply_last(c))
+        def multiply_last(c):
+            multiply_piece(3, 1, cols(c))
+
+            @pl.when(functools.reduce(jnp.logical_and, (c == PIECES // 2, me > 1, leads)))
+            def _():
+                for block in range(2):
+                    sent(0, block)
+                give_turn()
+
+        each(0, PIECES, multiply_last)
         each(split, n, attend)
 
         @pl.when(is_lower)
         def _():
-            each(0, PIECES, lambda c: project(n - 1, 1, c))
+            each(0, PIECES, lambda c: project(n - 1, 1, cols(c)))
 
             def stream(k):
                 token = 2 + k // PIECES
@@ -577,12 +639,27 @@
                 def _():
                     pass_on(0, k - LAG)
 
-            each(0, 2 * PIECES, stream)
+            def stream_late(k):
+                @pl.when(k < 2 * PIECES)
+                def _():
+                    pass_on(2 + k // PIECES, lax.rem(k, PIECES))
+
+                @pl.when(k >= LATE)
+                def _():
+                    pass_on(0, k - LATE)
+
+            @pl.when(leads)
+            def _():
+                each(0, PIECES + LATE, stream_late)
+
+            @pl.when(follows)
+            def _():
+                each(0, 2 * PIECES, stream)
 
         @pl.when(jnp.logical_not(is_lower))
         def _():
             def out_piece(c):
-                project(1, 3, c)
+                project(1, 3, cols(c))
                 pass_on(0, c)
 
             each(0, PIECES, out_piece)
@@ -598,7 +675,7 @@
 
             each(0, PIECES + LAG, two)
 
-        drain_gather(0, jnp.where(leads, me + 2, 0))
+        drain_gather(jnp.where(leads, 2, 0), jnp.where(leads, n - 1, 0))
 
         def finish(c):
             for way in range(2):
@@ -637,7 +714,7 @@
     weights = (query_weight, key_weight, value_matrix, output_weight)
     return pl.pallas_call(
         functools.partial(chain_kernel, n),
-        out_shape=jax.ShapeDtypeStruct((rows, width), bf16),
+        out_shape=pltpu.VMEM((rows, width), bf16),
         in_specs=[hbm] * 9,
         out_specs=vmem,
         scratch_shapes=[

time: 62.1 us -> 58.2 us (0.937)
  the two profiles are of different devices: /device:TPU:21 before, /device:TPU:23 now
where the time goes in v2:
time: 58.2 us; the launch traced here: 58.1 us
  Pallas kernels  57.3 us (98%)
  local copies, waits for them, and re-layouts  0.8 us (1%)
    pallas_call x1, Pallas kernels, fused(): pl.pallas_call(functools.partial(chain_kernel, n), out_shape=pltpu.VMEM((...  57.3 us

profile of v2, /device:TPU:23, one launch (start us, length us, event | category | flops | bytes accessed | tf_op | source)
XLA Modules:
  0.0 58.1 jit_solution(715608545821872093)
XLA Ops:
  0.0 57.3 %shard_map.91 = bf16[64,4096]{1,0:T(8,128)(2,1)S(1)} custom-call(bf16[64,4096]{1,0:T(8,128)(2,1)} %x_hbm.1, f32[1,4096]{1,0:T(1,128)} %bitcast.2, s32[4,4,8]{2,1,0:T(4,128)} %bitcast.3, f32[256,128]{1,0:T(8,128)} %constant.4.clone.cos_hbm, f32[256,128]{1,0:T(8,128)} %constant.5.clone.sin_hbm, bf16[4096,1024]{1,0:T(8,128)(2,1)} %wq_hbm.1, ...), custom_call_target="tpu_custom_call" | custom-call | tf_op jit(solution)/shard_map/pallas_call | solution.py:715
  57.3 0.8 %copy.11 = bf16[64,4096]{1,0:T(8,128)(2,1)} copy(bf16[64,4096]{1,0:T(8,128)(2,1)S(1)} %shard_map.91) | data formatting | bytes 1048576

commit v3 on v2

--- a/solution.py
+++ b/solution.py
@@ -162,7 +162,7 @@
 PIECES = 8
 SLOT = 4
 LAG = 4
-LATE = 16
+TURN = 3
 
 
 def chain_kernel(
@@ -208,14 +208,13 @@
     heads = wq.shape[1] // HEAD_SIZE
     kv_heads = wk.shape[1] // HEAD_SIZE
     group = heads // kv_heads
-    blocks = keep_ref.shape[1]
     has_left = me > 0
     has_right = me < n - 1
     is_lower = me < n // 2
     is_end = jnp.logical_or(me == 0, me == n - 1)
     pair = lax.axis_index("dp")
-    leads = lax.rem(pair, 2) == 0
-    partner = jnp.where(leads, pair + 1, pair - 1)
+    leads = lax.rem(pair, 2) == 1
+    partner = jnp.where(leads, pair - 1, pair + 1)
 
     loads = [
         pltpu.make_async_copy(src, dst, load_sem.at[i])
@@ -268,13 +267,16 @@
     def pairs(k):
         return pl.ds(pl.multiple_of(k * 2 * step, 2 * step), 2 * step)
 
+    def other(device, block):
+        return jnp.where(block > device, block - 1, block)
+
     def gather_copy(way, block, c):
         to = me + 1 - 2 * way
         return pltpu.make_async_remote_copy(
             src_ref=gathered.at[slot(me, block), :, cols(c)],
             dst_ref=gathered.at[slot(to, block), :, cols(c)],
-            send_sem=ag_send.at[way, block],
-            recv_sem=ag_recv.at[block, c],
+            send_sem=ag_send.at[block + way],
+            recv_sem=ag_recv.at[other(to, block), c],
             device_id={"tensor": to},
             device_id_type=MESH,
         )
@@ -287,8 +289,8 @@
         pltpu.make_async_remote_copy(
             src_ref=piece,
             dst_ref=piece,
-            send_sem=ag_send.at[0, 0],
-            recv_sem=ag_recv.at[block, c],
+            send_sem=ag_send.at[0],
+            recv_sem=ag_recv.at[other(me, block), c],
             device_id={"tensor": jnp.where(has_right, me + 1, me - 1)},
             device_id_type=MESH,
         ).wait_recv()
@@ -296,9 +298,9 @@
     def sum_copy(way, token, c):
         return pltpu.make_async_remote_copy(
             src_ref=parts.at[token, :, cols(c)],
-            dst_ref=incoming.at[way, token, :, cols(c)],
+            dst_ref=incoming.at[token + 1 - way, :, cols(c)],
             send_sem=rs_send.at[token],
-            recv_sem=rs_recv.at[way, token, c],
+            recv_sem=rs_recv.at[token + 1 - way, c],
             device_id={"tensor": me + 1 - 2 * way},
             device_id_type=MESH,
         )
@@ -330,10 +332,7 @@
     pl.when(leads)(send_own)
 
     def take_turn():
-        @pl.when(jnp.logical_not(leads))
-        def _():
-            pl.semaphore_wait(turn, 1)
-            send_own()
+        pl.semaphore_wait(turn, 1)
 
     def give_turn():
         pl.semaphore_signal(turn, inc=1, device_id={"dp": partner}, device_id_type=MESH)
@@ -358,15 +357,23 @@
             at += weight.shape[1]
         return spans
 
-    def multiply_whole(first):
-        for span, product in multiply(first, 1, slice(None)):
-            projected[pl.ds(first, 1), :, span] = product
+    def multiply_whole(first, between):
+        block = gathered[first]
+        at = 0
+        for weight in (wq, wk, wv):
+            span = slice(at, at + weight.shape[1])
+            projected[first, :, span] = jnp.dot(
+                block, weight[...], preferred_element_type=jnp.float32
+            )
+            if at == 0:
+                between()
+            at += weight.shape[1]
 
     def multiply_piece(first, count, where):
         for span, product in multiply(first, count, where):
             projected[pl.ds(first, count), :, span] += product
 
-    def attend_block(token):
+    def attend_block(token, length=length):
         here = slot(me, token)
         first_row = pl.multiple_of(token * rows, rows)
         where = pl.ds(first_row, rows)
@@ -392,10 +399,10 @@
         column = lax.broadcasted_iota(jnp.int32, (rows, length), 1)
         row = lax.broadcasted_iota(jnp.int32, (rows, length), 0) + first_row
         causal = column <= row
-        which = lax.broadcasted_iota(jnp.int32, (1, length), 1) // (length // blocks)
+        which = lax.broadcasted_iota(jnp.int32, (1, length), 1) // BLOCK
         for g in range(kv_heads):
             scores = lax.dot_general(
-                queries[g], keys[g], (((1,), (1,)), ((), ())), preferred_element_type=jnp.float32
+                queries[g], keys[g, :length], (((1,), (1,)), ((), ())), preferred_element_type=jnp.float32
             ) * np.float32(1.0 / np.sqrt(HEAD_SIZE))
             dropped = []
             for h in range(group):
@@ -404,12 +411,12 @@
                 terms = jnp.exp(one - highest)
                 inverse = 1.0 / (jnp.sum(terms, axis=-1, keepdims=True) * jnp.float32(0.9))
                 keeper = jnp.zeros((1, length), jnp.float32)
-                for j in range(blocks):
+                for j in range(length // BLOCK):
                     bit = keep_ref[token, j, g * group + h].astype(jnp.float32)
                     keeper = jnp.where(which == j, bit, keeper)
                 dropped.append((terms * inverse * keeper).astype(jnp.bfloat16))
             result = jnp.dot(
-                jnp.concatenate(dropped, axis=0), values[g], preferred_element_type=jnp.float32
+                jnp.concatenate(dropped, axis=0), values[g, :length], preferred_element_type=jnp.float32
             ).astype(jnp.bfloat16)
             for h in range(group):
                 at = (g * group + h) * HEAD_SIZE
@@ -427,7 +434,7 @@
         way = jnp.where(me < token, 0, 1)
         sum_copy(way, token, c).wait_recv()
         total = parts[token, :, cols(c)].astype(jnp.float32) + incoming[
-            way, token, :, cols(c)
+            token + 1 - way, :, cols(c)
         ].astype(jnp.float32)
         parts[token, :, cols(c)] = total.astype(jnp.bfloat16)
         sum_copy(way, token, c).start()
@@ -435,40 +442,43 @@
     keys[...] = jnp.zeros_like(keys)
     values[...] = jnp.zeros_like(values)
     projected[...] = jnp.zeros_like(projected)
-    for load in loads[3:6]:
-        load.wait()
+    def wait_inputs():
+        for load in loads[3:6]:
+            load.wait()
+
 
     def wait_tables():
         for load in loads[6:] + loads[2:3]:
             load.wait()
 
-    def drain_gather(early_up, early_down):
+    def drain_gather():
         def drain(block):
-            @pl.when(functools.reduce(jnp.logical_and, (block <= me, has_right, block >= early_up)))
+            @pl.when(jnp.logical_and(block <= me, has_right))
             def _():
                 sent(0, block)
 
-            @pl.when(functools.reduce(jnp.logical_and, (block >= me, has_left, block >= early_down)))
+            @pl.when(jnp.logical_and(block >= me, has_left))
             def _():
                 sent(1, block)
 
         each(0, n, drain)
 
     def sent(way, block):
-        whole_copy(gathered, ag_send.at[way, block], block).wait_send()
+        whole_copy(gathered, ag_send.at[block + way], block).wait_send()
 
     @pl.when(is_end)
     def _():
         way = jnp.where(me == 0, 0, 1)
-        multiply_whole(me)
+        wait_inputs()
+
+        @pl.when(jnp.logical_not(leads))
+        def _():
+            take_turn()
+            send_own()
+
+        multiply_whole(me, lambda: pl.when(leads)(give_turn))
         wait_tables()
 
-        @pl.when(jnp.logical_and(leads, me > 0))
-        def _():
-            sent(1, me)
-            give_turn()
-
-        take_turn()
         ahead = jnp.where(jnp.logical_and(leads, me > 0), n - 2, -1)
 
         def stream(i):
@@ -488,12 +498,13 @@
             def _():
                 stream(i)
 
-            attend_block(i)
-
-            @pl.when(functools.reduce(jnp.logical_and, (i == 0, me == 0, leads)))
-            def _():
-                sent(0, 0)
-                give_turn()
+            @pl.when(i == 0)
+            def _():
+                attend_block(0, rows)
+
+            @pl.when(i > 0)
+            def _():
+                attend_block(i)
 
             def out_piece(k):
                 project(i, 1, pairs(k))
@@ -512,14 +523,14 @@
             project(me, 1, pairs(k))
 
         each(0, PIECES // 2, out_own)
-        drain_gather(jnp.where(leads, n, 0), jnp.where(leads, n, 0))
+        drain_gather()
 
         def finish(c):
             sum_copy(1 - way, me, c).wait_recv()
             out_ref[:, cols(c)] = (
                 x_ref[:, cols(c)].astype(jnp.float32)
                 + parts[me, :, cols(c)].astype(jnp.float32)
-                + incoming[1 - way, me, :, cols(c)].astype(jnp.float32)
+                + incoming[me + way, :, cols(c)].astype(jnp.float32)
             ).astype(out_ref.dtype)
 
         each(0, PIECES, finish)
@@ -528,7 +539,9 @@
     def _():
         last = jnp.where(is_lower, n - 1, 1)
         last_way = jnp.where(is_lower, 1, 0)
-        skew = jnp.where(leads, (me - 1) * 2, 0)
+        up_lag = jnp.where(is_lower, 0, 3)
+        down_lag = jnp.where(is_lower, 2, 0)
+        lag = up_lag + down_lag
         split = jnp.where(is_lower, n - 1, 1)
         share = PIECES // SLOT
         follows = jnp.logical_not(leads)
@@ -542,33 +555,43 @@
         @pl.when(leads)
         def _():
             def both(c):
-                @pl.when(c < PIECES)
-                def _():
-                    forward(1, me + 1, c)
-
-                @pl.when(jnp.logical_and(c == PIECES // 2, me > 1))
-                def _():
-                    sent(1, me)
-                    give_turn()
-
-                @pl.when(c >= skew)
-                def _():
-                    forward(0, 0, c - skew)
-                    multiply_three(c - skew)
-
-            each(0, PIECES + skew, both)
+                @pl.when(jnp.logical_and(c >= up_lag, c < PIECES + up_lag))
+                def _():
+                    forward(0, 0, c - up_lag)
+
+                @pl.when(jnp.logical_and(c >= down_lag, c < PIECES + down_lag))
+                def _():
+                    forward(1, me + 1, c - down_lag)
+
+                @pl.when(jnp.logical_and(c == PIECES, is_lower))
+                def _():
+                    rest_of_own()
+
+                @pl.when(c == lag)
+                def _():
+                    wait_inputs()
+
+                @pl.when(c >= lag)
+                def _():
+                    multiply_three(c - lag)
+
+            each(0, PIECES + lag, both)
+
+            pl.when(me > 1)(give_turn)
+
 
         @pl.when(follows)
         def _():
-            take_turn()
+            wait_inputs()
             way = jnp.where(is_lower, 0, 1)
             first = jnp.where(is_lower, 0, n - 1)
             second = jnp.where(is_lower, 2, 0)
+            take_turn()
+            pl.when(me > 1)(send_own)
             each(0, PIECES, lambda c: forward(way, first, c))
-
-            @pl.when(me > 1)
-            def _():
-                pl.semaphore_wait(turn, 1)
+            pl.when(is_lower)(rest_of_own)
+            take_turn()
+            pl.when(is_lower)(send_own)
 
             def then(c):
                 forward(1 - way, second, c)
@@ -580,20 +603,14 @@
 
         @pl.when(is_lower)
         def _():
-            rest_of_own()
-
             def attend_forward(i):
                 attend(i)
                 each(i * share, (i + 1) * share, lambda c: forward(1, n - 1, c))
-
-                @pl.when(jnp.logical_and(i == 1, leads))
-                def _():
-                    for block in range(2):
-                        sent(0, block)
-                        sent(1, block + 1)
-                    give_turn()
+                pl.when(jnp.logical_and(i == 0, leads))(give_turn)
 
             each(0, n - 1, attend_forward)
+            pl.when(follows)(give_turn)
+
 
             def out_piece(c):
                 project(0, 3, cols(c))
@@ -602,30 +619,33 @@
                 def _():
                     forward(1, n - 1, c + (n - 1) * share)
 
+                pl.when(jnp.logical_and(c == TURN, leads))(give_turn)
+
             each(0, PIECES, out_piece)
 
+
         @pl.when(jnp.logical_not(is_lower))
         def _():
+            each(0, PIECES // 2, lambda c: forward(0, 1, c))
             attend(0)
 
             def out_piece(c):
+                @pl.when(c < PIECES // 2)
+                def _():
+                    forward(0, 1, c + PIECES // 2)
+
                 project(0, 1, cols(c))
-                forward(0, 1, c)
 
             each(0, PIECES, out_piece)
             rest_of_own()
+            pl.when(leads)(give_turn)
 
         def multiply_last(c):
             multiply_piece(3, 1, cols(c))
 
-            @pl.when(functools.reduce(jnp.logical_and, (c == PIECES // 2, me > 1, leads)))
-            def _():
-                for block in range(2):
-                    sent(0, block)
-                give_turn()
-
         each(0, PIECES, multiply_last)
         each(split, n, attend)
+
 
         @pl.when(is_lower)
         def _():
@@ -639,21 +659,17 @@
                 def _():
                     pass_on(0, k - LAG)
 
-            def stream_late(k):
-                @pl.when(k < 2 * PIECES)
-                def _():
-                    pass_on(2 + k // PIECES, lax.rem(k, PIECES))
-
-                @pl.when(k >= LATE)
-                def _():
-                    pass_on(0, k - LATE)
-
             @pl.when(leads)
             def _():
-                each(0, PIECES + LATE, stream_late)
+                take_turn()
+                each(0, PIECES, lambda c: pass_on(2, c))
+                each(0, PIECES, lambda c: pass_on(n - 1, c))
+                take_turn()
+                each(0, PIECES, lambda c: pass_on(0, c))
 
             @pl.when(follows)
             def _():
+                give_turn()
                 each(0, 2 * PIECES, stream)
 
         @pl.when(jnp.logical_not(is_lower))
@@ -661,6 +677,7 @@
             def out_piece(c):
                 project(1, 3, cols(c))
                 pass_on(0, c)
+                pl.when(jnp.logical_and(c == 1, follows))(give_turn)
 
             each(0, PIECES, out_piece)
 
@@ -673,9 +690,17 @@
                 def _():
                     pass_on(n - 1, c - LAG)
 
-            each(0, PIECES + LAG, two)
-
-        drain_gather(jnp.where(leads, 2, 0), jnp.where(leads, n - 1, 0))
+            @pl.when(leads)
+            def _():
+                each(0, PIECES, lambda c: pass_on(1, c))
+                take_turn()
+                each(0, PIECES, lambda c: pass_on(n - 1, c))
+
+            @pl.when(follows)
+            def _():
+                each(0, PIECES + LAG, two)
+
+        drain_gather()
 
         def finish(c):
             for way in range(2):
@@ -683,8 +708,8 @@
             out_ref[:, cols(c)] = (
                 x_ref[:, cols(c)].astype(jnp.float32)
                 + parts[me, :, cols(c)].astype(jnp.float32)
-                + incoming[0, me, :, cols(c)].astype(jnp.float32)
-                + incoming[1, me, :, cols(c)].astype(jnp.float32)
+                + incoming[me + 1, :, cols(c)].astype(jnp.float32)
+                + incoming[me, :, cols(c)].astype(jnp.float32)
             ).astype(out_ref.dtype)
 
         each(0, PIECES, finish)
@@ -728,17 +753,17 @@
         + [
             pltpu.VMEM((n, rows, width), bf16),
             pltpu.VMEM((n, rows, width), bf16),
-            pltpu.VMEM((2, n, rows, width), bf16),
+            pltpu.VMEM((n + 1, rows, width), bf16),
             pltpu.VMEM((kv_heads, length, HEAD_SIZE), bf16),
             pltpu.VMEM((kv_heads, length, HEAD_SIZE), bf16),
             pltpu.VMEM((kv_heads, heads // kv_heads * rows, HEAD_SIZE), bf16),
             pltpu.VMEM((n, rows, heads * HEAD_SIZE), bf16),
             pltpu.VMEM((n, rows, (heads + 2 * kv_heads) * HEAD_SIZE), jnp.float32),
             pltpu.SemaphoreType.DMA((9,)),
-            pltpu.SemaphoreType.DMA((2, n)),
-            pltpu.SemaphoreType.DMA((n, PIECES)),
+            pltpu.SemaphoreType.DMA((n + 1,)),
+            pltpu.SemaphoreType.DMA((n - 1, PIECES)),
             pltpu.SemaphoreType.DMA((n,)),
-            pltpu.SemaphoreType.DMA((2, n, PIECES)),
+            pltpu.SemaphoreType.DMA((n + 1, PIECES)),
             pltpu.SemaphoreType.REGULAR,
         ],
         compiler_params=pltpu.CompilerParams(

time: 58.2 us -> 55.6 us (0.955)
  the two profiles are of different devices: /device:TPU:23 before, /device:TPU:28 now
where the time goes in v3:
time: 55.6 us; the launch traced here: 55.4 us
  Pallas kernels  54.6 us (98%)
  local copies, waits for them, and re-layouts  0.8 us (1%)
    pallas_call x1, Pallas kernels, fused(): pl.pallas_call(functools.partial(chain_kernel, n), out_shape=pltpu.VMEM((...  54.6 us

profile of v3, /device:TPU:28, one launch (start us, length us, event | category | flops | bytes accessed | tf_op | source)
XLA Modules:
  0.0 55.4 jit_solution(4718287489067713983)
XLA Ops:
  0.0 54.6 %shard_map.91 = bf16[64,4096]{1,0:T(8,128)(2,1)S(1)} custom-call(bf16[64,4096]{1,0:T(8,128)(2,1)} %x_hbm.1, f32[1,4096]{1,0:T(1,128)} %bitcast.2, s32[4,4,8]{2,1,0:T(4,128)} %bitcast.3, f32[256,128]{1,0:T(8,128)} %constant.4.clone.cos_hbm, f32[256,128]{1,0:T(8,128)} %constant.5.clone.sin_hbm, bf16[4096,1024]{1,0:T(8,128)(2,1)} %wq_hbm.1, ...), custom_call_target="tpu_custom_call" | custom-call | tf_op jit(solution)/shard_map/pallas_call | solution.py:740
  54.6 0.8 %copy.11 = bf16[64,4096]{1,0:T(8,128)(2,1)} copy(bf16[64,4096]{1,0:T(8,128)(2,1)S(1)} %shard_map.91) | data formatting | bytes 1048576

commit v4 on v3

--- a/solution.py
+++ b/solution.py
@@ -161,6 +161,7 @@
 CHAIN = 4
 PIECES = 8
 SLOT = 4
+HALVES = 2
 LAG = 4
 TURN = 3
 
@@ -305,6 +306,20 @@
             device_id_type=MESH,
         )
 
+    def half_cols(c, h):
+        size = step // HALVES
+        return pl.ds(pl.multiple_of(c * step + h * size, size), size)
+
+    def half_copy(c, h):
+        return pltpu.make_async_remote_copy(
+            src_ref=parts.at[n - 1, :, half_cols(c, h)],
+            dst_ref=incoming.at[n, :, half_cols(c, h)],
+            send_sem=rs_send.at[n - 1],
+            recv_sem=rs_recv.at[n + h, c],
+            device_id={"tensor": jnp.where(has_right, me + 1, me - 1)},
+            device_id_type=MESH,
+        )
+
     def whole_copy(buffer, sem, index):
         return pltpu.make_async_remote_copy(
             src_ref=buffer.at[index],
@@ -318,7 +333,7 @@
     def each(first, last, body):
         lax.fori_loop(first, last, lambda c, carry: (body(c), carry)[1], 0)
 
-    early = jnp.where(me == 0, PIECES, jnp.where(leads, me * PIECES // 2, 0))
+    early = jnp.where(me == 0, PIECES, jnp.where(leads, me * PIECES // 4, 0))
 
     def send_own():
         @pl.when(has_right)
@@ -442,6 +457,16 @@
     keys[...] = jnp.zeros_like(keys)
     values[...] = jnp.zeros_like(values)
     projected[...] = jnp.zeros_like(projected)
+    def pass_last(c):
+        for h in range(HALVES):
+            where = half_cols(c, h)
+            half_copy(c, h).wait_recv()
+            total = parts[n - 1, :, where].astype(jnp.float32) + incoming[n, :, where].astype(
+                jnp.float32
+            )
+            parts[n - 1, :, where] = total.astype(jnp.bfloat16)
+            half_copy(c, h).start()
+
     def wait_inputs():
         for load in loads[3:6]:
             load.wait()
@@ -479,7 +504,6 @@
         multiply_whole(me, lambda: pl.when(leads)(give_turn))
         wait_tables()
 
-        ahead = jnp.where(jnp.logical_and(leads, me > 0), n - 2, -1)
 
         def stream(i):
             def piece(k):
@@ -489,12 +513,8 @@
 
             each(0, PIECES // 2, piece)
 
-        @pl.when(ahead >= 0)
-        def _():
-            stream(ahead)
-
         def iteration(i, carry):
-            @pl.when(jnp.logical_and(i != me, i != ahead))
+            @pl.when(i != me)
             def _():
                 stream(i)
 
@@ -508,8 +528,18 @@
 
             def out_piece(k):
                 project(i, 1, pairs(k))
-                sum_copy(way, i, 2 * k).start()
-                sum_copy(way, i, 2 * k + 1).start()
+                longest = jnp.logical_and(me == 0, i == n - 1)
+
+                @pl.when(longest)
+                def _():
+                    for c in (2 * k, 2 * k + 1):
+                        for h in range(HALVES):
+                            half_copy(c, h).start()
+
+                @pl.when(jnp.logical_not(longest))
+                def _():
+                    for c in (2 * k, 2 * k + 1):
+                        sum_copy(way, i, c).start()
 
             @pl.when(i != me)
             def _():
@@ -526,7 +556,15 @@
         drain_gather()
 
         def finish(c):
-            sum_copy(1 - way, me, c).wait_recv()
+            @pl.when(me > 0)
+            def _():
+                for h in range(HALVES):
+                    half_copy(c, h).wait_recv()
+
+            @pl.when(me == 0)
+            def _():
+                sum_copy(1, me, c).wait_recv()
+
             out_ref[:, cols(c)] = (
                 x_ref[:, cols(c)].astype(jnp.float32)
                 + parts[me, :, cols(c)].astype(jnp.float32)
@@ -606,7 +644,7 @@
             def attend_forward(i):
                 attend(i)
                 each(i * share, (i + 1) * share, lambda c: forward(1, n - 1, c))
-                pl.when(jnp.logical_and(i == 0, leads))(give_turn)
+                pl.when(jnp.logical_and(i == 1, leads))(give_turn)
 
             each(0, n - 1, attend_forward)
             pl.when(follows)(give_turn)
@@ -652,8 +690,13 @@
             each(0, PIECES, lambda c: project(n - 1, 1, cols(c)))
 
             def stream(k):
-                token = 2 + k // PIECES
-                pass_on(token, lax.rem(k, PIECES))
+                @pl.when(k < PIECES)
+                def _():
+                    pass_on(2, k)
+
+                @pl.when(k >= PIECES)
+                def _():
+                    pass_last(k - PIECES)
 
                 @pl.when(jnp.logical_and(k >= LAG, k < PIECES + LAG))
                 def _():
@@ -663,7 +706,7 @@
             def _():
                 take_turn()
                 each(0, PIECES, lambda c: pass_on(2, c))
-                each(0, PIECES, lambda c: pass_on(n - 1, c))
+                each(0, PIECES, pass_last)
                 take_turn()
                 each(0, PIECES, lambda c: pass_on(0, c))
 
@@ -688,13 +731,13 @@
 
                 @pl.when(c >= LAG)
                 def _():
-                    pass_on(n - 1, c - LAG)
+                    pass_last(c - LAG)
 
             @pl.when(leads)
             def _():
                 each(0, PIECES, lambda c: pass_on(1, c))
                 take_turn()
-                each(0, PIECES, lambda c: pass_on(n - 1, c))
+                each(0, PIECES, pass_last)
 
             @pl.when(follows)
             def _():
@@ -763,7 +806,7 @@
             pltpu.SemaphoreType.DMA((n + 1,)),
             pltpu.SemaphoreType.DMA((n - 1, PIECES)),
             pltpu.SemaphoreType.DMA((n,)),
-            pltpu.SemaphoreType.DMA((n + 1, PIECES)),
+            pltpu.SemaphoreType.DMA((n + HALVES, PIECES)),
             pltpu.SemaphoreType.REGULAR,
         ],
         compiler_params=pltpu.CompilerParams(

time: 55.6 us -> 55.5 us (level)
  no operation moved by 1% of the time
where the time goes in v4:
time: 55.5 us; the launch traced here: 55.3 us
  Pallas kernels  54.5 us (98%)
  local copies, waits for them, and re-layouts  0.8 us (1%)
    pallas_call x1, Pallas kernels, fused(): pl.pallas_call(functools.partial(chain_kernel, n), out_shape=pltpu.VMEM((...  54.5 us

profile of v4, /device:TPU:28, one launch (start us, length us, event | category | flops | bytes accessed | tf_op | source)
XLA Modules:
  0.0 55.3 jit_solution(6862542479646932531)
XLA Ops:
  0.0 54.5 %shard_map.91 = bf16[64,4096]{1,0:T(8,128)(2,1)S(1)} custom-call(bf16[64,4096]{1,0:T(8,128)(2,1)} %x_hbm.1, f32[1,4096]{1,0:T(1,128)} %bitcast.2, s32[4,4,8]{2,1,0:T(4,128)} %bitcast.3, f32[256,128]{1,0:T(8,128)} %constant.4.clone.cos_hbm, f32[256,128]{1,0:T(8,128)} %constant.5.clone.sin_hbm, bf16[4096,1024]{1,0:T(8,128)(2,1)} %wq_hbm.1, ...), custom_call_target="tpu_custom_call" | custom-call | tf_op jit(solution)/shard_map/pallas_call | solution.py:783
  54.5 0.8 %copy.11 = bf16[64,4096]{1,0:T(8,128)(2,1)} copy(bf16[64,4096]{1,0:T(8,128)(2,1)S(1)} %shard_map.91) | data formatting | bytes 1048576

commit v5 on v4

--- a/solution.py
+++ b/solution.py
@@ -161,7 +161,7 @@
 CHAIN = 4
 PIECES = 8
 SLOT = 4
-HALVES = 2
+HALVES = 1
 LAG = 4
 TURN = 3
 
@@ -644,7 +644,7 @@
             def attend_forward(i):
                 attend(i)
                 each(i * share, (i + 1) * share, lambda c: forward(1, n - 1, c))
-                pl.when(jnp.logical_and(i == 1, leads))(give_turn)
+                pl.when(jnp.logical_and(i == 0, leads))(give_turn)
 
             each(0, n - 1, attend_forward)
             pl.when(follows)(give_turn)

time: 55.5 us -> 55.6 us (level)
  no operation moved by 1% of the time
where the time goes in v5:
time: 55.6 us; the launch traced here: 55.5 us
  Pallas kernels  54.7 us (98%)
  local copies, waits for them, and re-layouts  0.8 us (1%)
    pallas_call x1, Pallas kernels, fused(): pl.pallas_call(functools.partial(chain_kernel, n), out_shape=pltpu.VMEM((...  54.7 us

profile of v5, /device:TPU:28, one launch (start us, length us, event | category | flops | bytes accessed | tf_op | source)
XLA Modules:
  0.0 55.5 jit_solution(7354087278127988922)
XLA Ops:
  0.0 54.7 %shard_map.91 = bf16[64,4096]{1,0:T(8,128)(2,1)S(1)} custom-call(bf16[64,4096]{1,0:T(8,128)(2,1)} %x_hbm.1, f32[1,4096]{1,0:T(1,128)} %bitcast.2, s32[4,4,8]{2,1,0:T(4,128)} %bitcast.3, f32[256,128]{1,0:T(8,128)} %constant.4.clone.cos_hbm, f32[256,128]{1,0:T(8,128)} %constant.5.clone.sin_hbm, bf16[4096,1024]{1,0:T(8,128)(2,1)} %wq_hbm.1, ...), custom_call_target="tpu_custom_call" | custom-call | tf_op jit(solution)/shard_map/pallas_call | solution.py:783
  54.7 0.8 %copy.11 = bf16[64,4096]{1,0:T(8,128)(2,1)} copy(bf16[64,4096]{1,0:T(8,128)(2,1)S(1)} %shard_map.91) | data formatting | bytes 1048576
